TPU v7x, 32 devices: a whole 2x2x4 slice. The times are simulated.
32 devices in a mesh: dp: 2 (over x), lon: 4 (over z), lat: 4 (over y, core).
Axes of the slice: x: 2, y: 2, z: 4, core: 2. Of those that a mesh axis runs over, the one named last changes fastest.
Arguments:
- grid_in: bfloat16 [32, 64, 64, 474], P('dp', 'lat', 'lon'), parts along dimension 0
- mesh_in: bfloat16 [128, 3], P(('lat', 'lon'))
- edge_in: bfloat16 [128, 48, 4], P(('lat', 'lon'))
- senders: int32 [128, 48], P(('lat', 'lon'))
- edge_mask: int32 [128, 48], P(('lat', 'lon'))
- w_grid: bfloat16 [474, 512], replicated
- w_mesh: bfloat16 [3, 512], replicated
- w_edge: bfloat16 [4, 512], replicated
- w_msg: bfloat16 [1536, 512], replicated
- w_node: bfloat16 [1024, 512], replicated
- w_gupd: bfloat16 [512, 512], replicated
- w_out: bfloat16 [6, 512, 512], replicated
- bias_gain: float32 [6, 4, 512], replicated
Outputs:
- output 1: bfloat16 [32, 128, 512], P('dp', ('lat', 'lon')), parts along dimension 0
- output 2: bfloat16 [32, 64, 64, 512], P('dp', 'lat', 'lon'), parts along dimension 0
There are 2 independent parts. A program takes and returns all parts, laid end to end along the dimension named above; an argument that names none is the same for every part.
All inputs are finite; a program needn't handle non-finite values.
Results may differ from a plain program's by a relative error of at most 0.00871152.
Values are sent between devices in bfloat16 or wider.
A program may use at most 1 GiB of HBM per device.

v0:
```python
import functools

import jax
import jax.numpy as jnp
from jax import lax
from jax.experimental import pallas as pl
from jax.experimental.pallas import tpu as pltpu
from jax.sharding import PartitionSpec as P

REACH = 3
LN_EPS = 1e-5
FEATS = 16
TILE = 32
SUB = 256
LP = None
PREP = 128
CODE = 64
PACK_VMEM = 40 * 2 ** 20
PACK_FLOPS = 2 * 10 ** 9
PACK_BYTES = 10 ** 6
EDGE_VMEM = 20 * 2 ** 20
NODE_VMEM = 6 * 2 ** 20
GRID_VMEM = 24 * 2 ** 20
UPDATE_VMEM = 12 * 2 ** 20
F32 = jnp.float32
BF16 = jnp.bfloat16


def mm(a, b):
    return jnp.dot(a, b, preferred_element_type=F32)


def mm_nt(a, b):
    return lax.dot_general(a, b, (((1,), (1,)), ((), ())), preferred_element_type=F32)


def gate(t):
    return (t + t * jnp.tanh(t)).astype(BF16)


def swish(x):
    return gate(x * 0.5)


def norm(y):
    scale = 1.0 / y.shape[-1]
    centered = y - jnp.sum(y, axis=-1, keepdims=True) * scale
    var = jnp.sum(centered * centered, axis=-1, keepdims=True) * scale
    return centered * lax.rsqrt(var + LN_EPS)


def mlp_tail(pre, w2, bg):
    y = mm(swish(pre), w2) + bg[1:2]
    return norm(y) * bg[2:3] + bg[3:4]


def swap_rows(value, scr, inner, put):
    outer = value.shape[0] // inner
    pitch = scr.shape[1] // outer
    for k in range(scr.shape[0]):
        for b in range(outer):
            scr[k, pl.ds(b * pitch, inner), :] = value[b * inner:(b + 1) * inner, 128 * k:128 * (k + 1)]
    for c in range(inner):
        for k in range(scr.shape[0]):
            put(c, k, scr[k, pl.ds(c, outer, stride=pitch), :].astype(BF16))


def pack_slots(send_ref, mask_ref, edge_ref, mesh_ref, lanes, table, lon, grid_cols):
    nodes, per_node = send_ref.shape
    bits = grid_cols.bit_length() - 1
    send = send_ref[...]
    row = lax.shift_right_logical(send, bits).astype(F32)
    col = (send & (grid_cols - 1)).astype(F32)
    mask = mask_ref[...].astype(F32)
    mesh = mesh_ref[...].astype(F32)
    pieces = []
    for n in range(nodes):
        here = slice(n, n + 1)
        lanes[...] = jnp.zeros_like(lanes)
        lanes[0:4, 0:per_node] = edge_ref[n].astype(F32)
        lanes[4:5, 0:per_node] = row[here]
        lanes[5:6, 0:per_node] = col[here]
        lanes[6:7, 0:per_node] = mask[here]
        lanes[7:8, 0:per_node] = jnp.full((1, per_node), n, F32) + (lon * nodes).astype(F32)
        lanes[8:11, 0:per_node] = jnp.broadcast_to(mesh[:, here], (3, per_node))
        pieces.append(lanes[...])
    for p in range(nodes // 2):
        table[:, 128 * p:128 * (p + 1)] = pieces[p] + pltpu.roll(pieces[p + nodes // 2], 64, 1)


def idle_kernel(out_ref):
    out_ref[...] = jnp.zeros_like(out_ref)


def idle_call():
    return pl.pallas_call(
        idle_kernel,
        out_shape=jax.ShapeDtypeStruct((8, 128), F32),
        compiler_params=pltpu.CompilerParams(vmem_limit_bytes=PACK_VMEM),
        cost_estimate=pl.CostEstimate(flops=PACK_FLOPS, transcendentals=0, bytes_accessed=PACK_BYTES),
        name='idle',
    )()


def pack_kernel(send_ref, mask_ref, edge_ref, mesh_ref, dep_ref, wm_ref, wo_ref, bg_ref, out_ref, vm_ref, lanes, table, *, grid_cols):
    pack_slots(send_ref, mask_ref, edge_ref, mesh_ref, lanes, table, lax.axis_index('lon'), grid_cols)
    out_ref[...] = table[...].astype(BF16)
    latent = wo_ref.shape[-1]
    nodes = mesh_ref.shape[1]
    feat = jnp.concatenate([mesh_ref[...].astype(F32), jnp.zeros((nodes - 3, nodes), F32)], axis=0)
    weight = jnp.concatenate([wm_ref[...].astype(F32), jnp.zeros((nodes - 3, latent), F32)], axis=0)
    pre = lax.dot_general(
        feat.astype(BF16), weight.astype(BF16), (((0,), (0,)), ((), ())), preferred_element_type=F32)
    bg1 = bg_ref[1]
    vm_ref[...] = mlp_tail(pre + bg1[0:1], wo_ref[1], bg1).astype(BF16).astype(F32)


def pack_call(senders, edge_mask, edge_t, mesh_t, dep, w_mesh, w_out, bias_gain, grid_cols):
    width = senders.shape[0] // 2 * 128
    latent = w_out.shape[-1]
    return pl.pallas_call(
        functools.partial(pack_kernel, grid_cols=grid_cols),
        out_shape=[jax.ShapeDtypeStruct((FEATS, width), BF16), jax.ShapeDtypeStruct((senders.shape[0], latent), F32)],
        scratch_shapes=[pltpu.VMEM((FEATS, 128), F32), pltpu.VMEM((FEATS, width), F32)],
        compiler_params=pltpu.CompilerParams(vmem_limit_bytes=PACK_VMEM),
        cost_estimate=pl.CostEstimate(flops=PACK_FLOPS, transcendentals=0, bytes_accessed=PACK_BYTES),
        name='pack',
    )(senders, edge_mask, edge_t, mesh_t, dep, w_mesh, w_out, bias_gain)


def rank_slots(vtb, lon, cols, nodes):
    slots = vtb.shape[1]
    chunks = slots // 128
    vt = vtb.astype(F32)
    col = vt[5:6] - (lon * cols).astype(F32)
    cell = vt[7:8] - (lon * nodes).astype(F32)
    inner = (cell > -0.5) & (cell < nodes - 0.5)
    live = (vt[6:7] > 0.5) & (col > -0.5) & (col < cols - 0.5)
    up = lax.broadcasted_iota(jnp.int32, (128, 128), 0) <= lax.broadcasted_iota(jnp.int32, (128, 128), 1)
    low = lax.broadcasted_iota(jnp.int32, (chunks, chunks), 1) < lax.broadcasted_iota(jnp.int32, (chunks, chunks), 0)
    up = jnp.where(up, 1.0, 0.0).astype(BF16)
    low = jnp.where(low, 1.0, 0.0).astype(BF16)
    ones = jnp.full((chunks, chunks), 1.0, BF16)

    def count(flag):
        flag = jnp.where(flag, 1.0, 0.0)
        flags = jnp.concatenate([flag[:, 128 * c:128 * (c + 1)] for c in range(chunks)], axis=0)
        incl = mm(flags.astype(BF16), up)
        row_sum = jnp.broadcast_to(incl[:, 127:128], (chunks, 128)).astype(BF16)
        return flags, incl + mm(low, row_sum) - 1.0, mm(ones, row_sum)

    far, far_rank, n_far = count(live & jnp.logical_not(inner))
    near, near_rank, n_near = count(live & inner)
    skip = jnp.floor((n_far + (TILE - 1)) * (1.0 / TILE)) * TILE
    rank = jnp.where(far > 0.5, far_rank, jnp.where(near > 0.5, near_rank + skip, -1.0))
    return rank, n_far, skip + n_near


def embed_kernel(x_ref, wg_ref, wo_ref, bg_ref, feat_ref, own_vm_ref,
                 vg_ref, tab_ref, band_ref, rank_ref, vm_ref,
                 scr, half, from_south, from_north, feat_in, vm_in, up_sems, down_sems, feat_send, feat_recv, vm_send, vm_recv, *, lats, lons):
    batch, grid_rows, cols, chans = x_ref.shape
    latent = vg_ref.shape[-1]
    lat = lax.axis_index('lat')
    lon = lax.axis_index('lon')
    odd = lax.rem(lat, 2)
    inner_north = lat > 0
    inner_south = lat < lats - 1
    mesh_id = pl.DeviceIdType.MESH

    def strip(start, dst, sems, to):
        return pltpu.make_async_remote_copy(
            tab_ref.at[pl.ds(start, REACH)], dst, sems.at[0], sems.at[1], device_id={'lat': to}, device_id_type=mesh_id)

    north_send = strip(REACH, from_south, up_sems, lat - 1)
    south_send = strip(grid_rows, from_north, down_sems, lat + 1)
    feats = [pltpu.make_async_remote_copy(
        feat_ref, feat_in.at[lon], feat_send.at[k - 1], feat_recv.at[k - 1],
        device_id={'lon': lax.rem(lon + k, lons)}, device_id_type=mesh_id) for k in range(1, lons)]
    feats += [pltpu.make_async_remote_copy(
        own_vm_ref, vm_in.at[lon], vm_send.at[k - 1], vm_recv.at[k - 1],
        device_id={'lon': lax.rem(lon + k, lons)}, device_id_type=mesh_id) for k in range(1, lons)]

    barrier = pltpu.get_barrier_semaphore()
    for k in range(1, lons):
        pl.semaphore_signal(barrier, 1, device_id={'lon': lax.rem(lon + k, lons)}, device_id_type=mesh_id)

    @pl.when(inner_north)
    def _():
        pl.semaphore_signal(barrier, 1, device_id={'lat': lat - 1}, device_id_type=mesh_id)

    @pl.when(inner_south)
    def _():
        pl.semaphore_signal(barrier, 1, device_id={'lat': lat + 1}, device_id_type=mesh_id)

    feat_in[lon] = feat_ref[...]
    vm_in[lon] = own_vm_ref[...]
    half[...] = wg_ref[...] * jnp.asarray(0.5, BF16)
    bg = bg_ref[0]
    b1 = bg[0:1] * 0.5

    def row(i):
        return i + odd * (grid_rows - 1 - 2 * i)

    def first(i):
        return gate(mm(x_ref[:, row(i)].reshape(batch * cols, chans), half[...]) + b1)

    def second(i, hid):
        vg = norm(mm(hid, wo_ref[0]) + bg[1:2]) * bg[2:3] + bg[3:4]
        vg_ref[:, row(i)] = vg.astype(BF16).reshape(batch, cols, latent)

        def put(c, k, part):
            tab_ref[REACH + row(i), c, :, 128 * k:128 * (k + 1)] = part

        swap_rows(vg, scr.at[i % scr.shape[0]], cols, put)

    staged(range(REACH), first, second)
    pl.semaphore_wait(barrier, lons - 1 + inner_north.astype(jnp.int32) + inner_south.astype(jnp.int32))

    @pl.when(inner_north & (odd == 0))
    def _():
        north_send.start()

    @pl.when(inner_south & (odd == 1))
    def _():
        south_send.start()

    for copy in feats:
        copy.start()
    middle = grid_rows // 2
    staged(list(range(grid_rows - REACH, grid_rows)) + list(range(REACH, middle)), first, second)

    @pl.when(inner_north & (odd == 1))
    def _():
        north_send.start()

    @pl.when(inner_south & (odd == 0))
    def _():
        south_send.start()

    def extra():
        band_ref[...] = feat_in[...]
        vtb = jnp.concatenate([feat_in[k] for k in range(lons)], axis=1)
        nodes = 2 * (feat_in.shape[2] // 128)
        rank, n_far, end = rank_slots(vtb, lon, cols, nodes)
        rank_ref[0:rank.shape[0]] = rank
        rank_ref[rank.shape[0]:rank.shape[0] + 8] = n_far[0:8]
        rank_ref[rank.shape[0] + 8:] = end[0:8]
        vm_ref[...] = vm_in[...].reshape(lons * nodes, latent)

    for copy in feats:
        copy.wait()
    staged(range(middle, grid_rows - REACH), first, second, extra)

    @pl.when(inner_north)
    def _():
        north_send.wait_send()
        south_send.wait_recv()
        tab_ref[0:REACH] = from_north[...]

    @pl.when(inner_south)
    def _():
        south_send.wait_send()
        north_send.wait_recv()
        tab_ref[grid_rows + REACH:grid_rows + 2 * REACH] = from_south[...]


def embed_call(grid_in, w_grid, w_out, bias_gain, feats, own_vm, lats, lons):
    batch, rows, cols, chans = grid_in.shape
    latent = w_out.shape[-1]
    strip = (REACH, cols, batch, latent)
    local = pl.BlockSpec(memory_space=pltpu.VMEM)
    return pl.pallas_call(
        functools.partial(embed_kernel, lats=lats, lons=lons),
        in_specs=[local] * 6,
        out_specs=[local] * 5,
        out_shape=[
            jax.ShapeDtypeStruct((batch, rows, cols, latent), BF16),
            jax.ShapeDtypeStruct((rows + 2 * REACH, cols, batch, latent), BF16),
            jax.ShapeDtypeStruct((lons,) + feats.shape, BF16),
            jax.ShapeDtypeStruct((lons * feats.shape[1] // 128 + 16, 128), F32),
            jax.ShapeDtypeStruct((lons * feats.shape[1] // 64, latent), F32)],
        scratch_shapes=[
            pltpu.VMEM((4, latent // 128, batch * (cols + 8), 128), F32),
            pltpu.VMEM((chans, latent), BF16),
            pltpu.VMEM(strip, BF16), pltpu.VMEM(strip, BF16),
            pltpu.VMEM((lons,) + feats.shape, BF16), pltpu.VMEM((lons,) + own_vm.shape, F32),
            pltpu.SemaphoreType.DMA((2,)), pltpu.SemaphoreType.DMA((2,)),
            pltpu.SemaphoreType.DMA((lons - 1,)), pltpu.SemaphoreType.DMA((lons - 1,)),
            pltpu.SemaphoreType.DMA((lons - 1,)), pltpu.SemaphoreType.DMA((lons - 1,))],
        compiler_params=pltpu.CompilerParams(collective_id=0, has_side_effects=True, vmem_limit_bytes=GRID_VMEM),
        cost_estimate=pl.CostEstimate(
            flops=4 * rows * batch * cols * latent * latent, transcendentals=0,
            bytes_accessed=6 * rows * batch * cols * latent),
        name='embed',
    )(grid_in, w_grid, w_out, bias_gain, feats, own_vm)


def staged(items, first, second, extra=None):
    items = list(items)
    hid = first(items[0])
    if extra is not None:
        extra()
    for k, item in enumerate(items):
        nxt = first(items[k + 1]) if k + 1 < len(items) else None
        second(item, hid)
        hid = nxt


def update_kernel(vg_ref, wu_ref, wo_ref, bg_ref, dep_ref, out_ref, half, obuf, sems):
    half[...] = wu_ref[...] * jnp.asarray(0.5, BF16)
    bg = bg_ref[5]
    b1 = bg[0:1] * 0.5
    count = vg_ref.shape[0] // SUB

    def rows(i):
        return pl.ds(i * SUB, SUB)

    def put(i):
        return pltpu.make_async_copy(obuf.at[rows(i)], out_ref.at[rows(i)], sems.at[i])

    def first(i):
        return gate(mm(vg_ref[rows(i), :], half[...]) + b1)

    def second(i, hid):
        upd = norm(mm(hid, wo_ref[5]) + bg[1:2]) * bg[2:3] + bg[3:4]
        obuf[rows(i), :] = (vg_ref[rows(i), :].astype(F32) + upd).astype(BF16)
        if i:
            put(i - 1).start()

    staged(range(count), first, second)
    put(count - 1).start()
    for i in range(count):
        put(i).wait()


def update_call(vg, w_gupd, w_out, bias_gain, dep):
    rows, latent = vg.shape
    local = pl.BlockSpec(memory_space=pltpu.VMEM)
    anywhere = pl.BlockSpec(memory_space=pl.ANY)
    return pl.pallas_call(
        update_kernel,
        in_specs=[local] * 4 + [anywhere],
        out_specs=anywhere,
        out_shape=jax.ShapeDtypeStruct(vg.shape, BF16),
        scratch_shapes=[pltpu.VMEM((latent, latent), BF16), pltpu.VMEM(vg.shape, BF16), pltpu.SemaphoreType.DMA((rows // SUB,))],
        cost_estimate=pl.CostEstimate(flops=4 * rows * latent * latent, transcendentals=0, bytes_accessed=4 * rows * latent),
        compiler_params=pltpu.CompilerParams(vmem_limit_bytes=UPDATE_VMEM),
        name='update',
    )(vg, w_gupd, w_out, bias_gain, dep)


def spread(ref, base, count, reps):
    rows = []
    for s in range(count):
        row = jnp.concatenate([ref[k, pl.ds(base + s, 8, stride=0), :] for k in range(ref.shape[0])], axis=1)
        rows += [row] * reps
    return jnp.concatenate(rows, axis=0)


def put_lanes(ref, rows, value):
    for k in range(ref.shape[0]):
        ref[k, rows, :] = value[:, 128 * k:128 * (k + 1)]


def message_loop(start, stop, tab_ref, w_in, w3, bg3, lp, ec, idx, part, bufs, hids):
    rows, cols, batch, latent = tab_ref.shape
    table = tab_ref.reshape(rows * cols, batch, latent)
    per = TILE // 2
    b2 = bg3[1:2]
    gain = bg3[2:3]

    def first(base, k):
        for s in range(per):
            bufs[k % 2][pl.ds(s * batch, batch), :] = table[lax.div(idx[0, base + s], CODE)]
        acc = mm(bufs[k % 2][...], w_in[...])
        hids[k][...] = gate(acc + spread(lp, base, per, batch // 8))

    def second(base, k):
        y = mm(hids[k][...], w3[...]) + b2
        z = norm(y) * gain + spread(ec, base, per, batch // 8)
        z = z.astype(BF16).astype(F32).reshape(per, batch, latent)
        for s in range(per):
            n = lax.rem(idx[0, base + s], CODE)
            part[n] += z[s]

    def both(t, k, stage):
        for j in range(2):
            stage(t * TILE + j * per, 2 * k + j)

    def mixed(t1, k1, t2, k2):
        for j in range(2):
            first(t1 * TILE + j * per, 2 * k1 + j)
            second(t2 * TILE + j * per, 2 * k2 + j)

    @pl.when(stop > start)
    def _():
        both(start, 0, first)

    def step(m, carry):
        t = start + 2 * m
        mixed(t + 1, 1, t, 0)
        mixed(jnp.minimum(t + 2, stop - 1), 0, t + 1, 1)
        return carry

    lax.fori_loop(0, lax.div(stop - start, 2), step, 0)

    @pl.when(lax.rem(stop - start, 2) == 1)
    def _():
        both(stop - 1, 0, second)


def three_parts(x):
    hi = x.astype(BF16)
    rest = x - hi.astype(F32)
    mid = rest.astype(BF16)
    return jnp.concatenate([hi, mid, (rest - mid.astype(F32)).astype(BF16)], axis=0)


def select(rank, base):
    slot = lax.broadcasted_iota(jnp.int32, (PREP, 128), 0).astype(F32) + base
    return jnp.concatenate(
        [jnp.where(rank[c:c + 1] == slot, 1.0, 0.0).astype(BF16) for c in range(rank.shape[0])], axis=1)


def prepare(start, stop, rank, vtb, we_ref, wmsg_ref, wo_ref, bg_ref, node_proj, lp, ec):
    latent = wo_ref.shape[-1]
    band = node_proj.shape[0] // 3
    we = jnp.concatenate([we_ref[...].astype(F32), jnp.zeros((FEATS - 4, latent), F32)], axis=0).astype(BF16)
    bg2 = bg_ref[2]
    bg3 = bg_ref[3]

    def prep(t, carry):
        feat = mm_nt(select(rank, (t * PREP).astype(F32)), vtb).astype(BF16)
        here = pl.ds(pl.multiple_of(t * PREP, PREP), PREP)
        edge = mlp_tail(mm(feat, we) + bg2[0:1], wo_ref[2], bg2).astype(BF16)
        lane = lax.rem(lax.broadcasted_iota(jnp.int32, (PREP, 3 * band), 1), band).astype(F32)
        hot = jnp.where(lane == feat[:, 7:8].astype(F32), 1.0, 0.0).astype(BF16)
        put_lanes(lp, here, (mm(edge, wmsg_ref[0:latent, :]) + mm(hot, node_proj[...]) + bg3[0:1]) * 0.5)
        put_lanes(ec, here, edge.astype(F32) + bg3[3:4])
        return carry

    lax.fori_loop(start, stop, prep, 0)


def far_kernel(v_ref, rank_ref, vm_ref, we_ref, wmsg_ref, wo_ref, bg_ref, tab_ref,
               p1_ref, p2_ref, p3_ref, idx_v, proj_ref,
               lp, ec, idx_s, part, half, hid_a, hid_b, hid_c, hid_d, buf_a, buf_b, isem, *, lons, nodes):
    latent = wo_ref.shape[-1]
    grid_rows, cols = tab_ref.shape[:2]
    positions = grid_rows * cols
    cell_rows = grid_rows - 2 * REACH
    band = lons * nodes
    chunks = rank_ref.shape[0] - 16
    meta = idx_v.shape[1] - 128
    lat = lax.axis_index('lat')
    lon = lax.axis_index('lon')
    vtb = jnp.concatenate([v_ref[k] for k in range(lons)], axis=1)
    rank = rank_ref[0:chunks]
    n_far = jnp.max(rank_ref[chunks:chunks + 8]).astype(jnp.int32)
    end = jnp.max(rank_ref[chunks + 8:]).astype(jnp.int32)
    far_tiles = lax.div(n_far + TILE - 1, TILE)
    skip = far_tiles * TILE
    proj_ref[...] = three_parts(mm(vm_ref[...].astype(BF16), wmsg_ref[2 * latent:, :]))

    def index(t, carry):
        feat_t = mm_nt(vtb, select(rank, (t * PREP).astype(F32)))
        here = pl.ds(pl.multiple_of(t * PREP, PREP), PREP)
        slot = lax.broadcasted_iota(jnp.int32, (1, PREP), 1) + t * PREP
        used = (slot < n_far) | ((slot >= skip) & (slot < end))
        win_r = feat_t[4:5] - (lat * cell_rows - REACH).astype(F32)
        win_c = feat_t[5:6] - (lon * cols).astype(F32)
        pos = jnp.clip(jnp.where(used, (win_r * cols + win_c).astype(jnp.int32), REACH * cols), 0, positions - 1)
        node = feat_t[7:8].astype(jnp.int32)
        cell = lax.div(node, nodes)
        rel = jnp.where(used, jnp.bitwise_xor(cell, lon) * nodes + (node - cell * nodes), band)
        idx_v[0:1, here] = pos * CODE + rel
        return carry

    lax.fori_loop(0, lax.div(end + PREP - 1, PREP), index, 0)
    lane = lax.broadcasted_iota(jnp.int32, (1, 128), 1)
    idx_v[0:1, meta:meta + 128] = jnp.where(lane == 0, far_tiles, lax.div(end + TILE - 1, TILE))
    move = pltpu.make_async_copy(idx_v, idx_s, isem)
    move.start()
    part[...] = jnp.zeros_like(part)
    half[...] = wmsg_ref[latent:2 * latent, :] * jnp.asarray(0.5, BF16)
    prepare(0, lax.div(skip + PREP - 1, PREP), rank, vtb, we_ref, wmsg_ref, wo_ref, bg_ref, proj_ref, lp, ec)
    move.wait()
    message_loop(0, far_tiles, tab_ref, half, wo_ref.at[3], bg_ref[3], lp, ec, idx_s, part, (buf_a, buf_b), (hid_a, hid_b, hid_c, hid_d))
    for k, ref in enumerate((p1_ref, p2_ref, p3_ref)):
        ref[...] = part[(k + 1) * nodes:(k + 2) * nodes]


def near_kernel(idx, v_ref, rank_ref, proj_ref, we_ref, wmsg_ref, wo_ref, bg_ref, tab_ref, own_ref, lp, ec, part, half, hid_a, hid_b, hid_c, hid_d, buf_a, buf_b):
    latent = wo_ref.shape[-1]
    nodes = own_ref.shape[0]
    part[...] = jnp.zeros_like(part)
    half[...] = wmsg_ref[latent:2 * latent, :] * jnp.asarray(0.5, BF16)
    vtb = jnp.concatenate([v_ref[k] for k in range(v_ref.shape[0])], axis=1)
    meta = idx.shape[1] - 128
    start, stop = idx[0, meta], idx[0, meta + 1]
    ratio = PREP // TILE
    prepare(lax.div(start, ratio), lax.div(stop + ratio - 1, ratio), rank_ref[0:rank_ref.shape[0] - 16], vtb, we_ref, wmsg_ref, wo_ref, bg_ref,
            proj_ref, lp, ec)
    message_loop(start, stop, tab_ref, half, wo_ref.at[3], bg_ref[3], lp, ec, idx, part,
                 (buf_a, buf_b), (hid_a, hid_b, hid_c, hid_d))
    own_ref[...] = part[0:nodes]


def loop_scratch(batch, latent):
    half_tile = pltpu.VMEM((TILE // 2 * batch, latent), BF16)
    return [pltpu.VMEM((latent, latent), BF16)] + [half_tile] * 6


def edge_call(v, rank, vm, w_edge, w_msg, w_out, bias_gain, table, lons, nodes, per_node):
    latent = w_out.shape[-1]
    batch = table.shape[2]
    limit = lons * nodes * per_node + PREP + 128
    local = pl.BlockSpec(memory_space=pltpu.VMEM)
    outs = [jax.ShapeDtypeStruct((nodes, batch, latent), F32)] * (lons - 1)
    outs += [jax.ShapeDtypeStruct((1, limit), jnp.int32), jax.ShapeDtypeStruct((3 * lons * nodes, latent), BF16)]
    res = pl.pallas_call(
        functools.partial(far_kernel, lons=lons, nodes=nodes),
        in_specs=[local] * 8,
        out_specs=[local] * len(outs),
        out_shape=outs,
        scratch_shapes=[
            pltpu.VMEM((latent // 128, limit, 128), F32), pltpu.VMEM((latent // 128, limit, 128), F32),
            pltpu.SMEM((1, limit), jnp.int32),
            pltpu.VMEM((lons * nodes + 1, batch, latent), F32)] + loop_scratch(batch, latent) + [pltpu.SemaphoreType.DMA],
        compiler_params=pltpu.CompilerParams(vmem_limit_bytes=EDGE_VMEM),
        cost_estimate=pl.CostEstimate(
            flops=4 * limit // 8 * batch * latent * latent, transcendentals=0, bytes_accessed=limit * batch * latent),
        name='edges_far',
    )(v, rank, vm, w_edge, w_msg, w_out, bias_gain, table)
    return res[:lons - 1], res[lons - 1:]


def near_call(v, rank, lists, w_edge, w_msg, w_out, bias_gain, table, nodes, band):
    idx, proj = lists
    latent = w_out.shape[-1]
    batch = table.shape[2]
    local = pl.BlockSpec(memory_space=pltpu.VMEM)
    return pl.pallas_call(
        near_kernel,
        in_specs=[pl.BlockSpec(memory_space=pltpu.SMEM)] + [local] * 8,
        out_specs=[local],
        out_shape=[jax.ShapeDtypeStruct((nodes, batch, latent), F32)],
        scratch_shapes=[pltpu.VMEM((latent // 128, idx.shape[1], 128), F32), pltpu.VMEM((latent // 128, idx.shape[1], 128), F32),
                        pltpu.VMEM((band + 1, batch, latent), F32)] + loop_scratch(batch, latent),
        compiler_params=pltpu.CompilerParams(vmem_limit_bytes=EDGE_VMEM),
        cost_estimate=pl.CostEstimate(
            flops=idx.shape[1] * batch * latent * latent, transcendentals=0, bytes_accessed=idx.shape[1] * batch * latent),
        name='edges_near',
    )(idx, v, rank, proj, w_edge, w_msg, w_out, bias_gain, table)


def node_kernel(own_ref, r1_ref, r2_ref, r3_ref, vm_ref, wn_ref, w4_ref, bg_ref, out_ref, scr):
    nodes, batch, latent = own_ref.shape
    agg = (own_ref[...] + r1_ref[...] + r2_ref[...] + r3_ref[...]).astype(BF16).reshape(nodes * batch, latent)
    bg = bg_ref[4]
    own_vm = vm_ref[...]
    base = mm(own_vm.astype(BF16), wn_ref[0:latent, :]) + bg[0:1]
    acc = mm(agg, wn_ref[latent:, :]).reshape(nodes, batch, latent) + base.reshape(nodes, 1, latent)
    upd = mlp_tail(acc.reshape(nodes * batch, latent), w4_ref[4], bg)
    out = (upd.reshape(nodes, batch, latent) + own_vm.reshape(nodes, 1, latent)).reshape(nodes * batch, latent)

    def put(b, k, part):
        out_ref[b, :, 128 * k:128 * (k + 1)] = part

    swap_rows(out, scr, batch, put)


def node_call(blocks, vm, w_node, w_out, bias_gain):
    nodes, batch, latent = blocks[0].shape
    local = pl.BlockSpec(memory_space=pltpu.VMEM)
    out = jax.ShapeDtypeStruct((batch, nodes, latent), BF16)
    return pl.pallas_call(
        node_kernel,
        in_specs=[local] * 8,
        out_specs=local,
        out_shape=out,
        compiler_params=pltpu.CompilerParams(vmem_limit_bytes=NODE_VMEM),
        scratch_shapes=[pltpu.VMEM((latent // 128, nodes * (batch + 8), 128), F32)],
        name='nodes',
    )(*blocks, vm, w_node, w_out, bias_gain)


def solution(mesh):
    lats = mesh.shape['lat']
    lons = mesh.shape['lon']
    south_shift = [(s, s + 1) for s in range(lats - 1)]
    north_shift = [(s + 1, s) for s in range(lats - 1)]

    def cell_step(grid_in, mesh_in, edge_in, senders, edge_mask, w_grid, w_mesh, w_edge, w_msg, w_node, w_gupd, w_out, bias_gain):
        batch, rows, cols, _ = grid_in.shape
        nodes = senders.shape[0]
        latent = w_out.shape[-1]
        feats, own_vm = pack_call(
            senders, edge_mask, jnp.swapaxes(edge_in, 1, 2), mesh_in.T, idle_call(), w_mesh, w_out, bias_gain, cols * lons)
        vg, table, band, rank, vm = embed_call(grid_in, w_grid, w_out, bias_gain, feats, own_vm, lats, lons)
        blocks, lists = edge_call(band, rank, vm, w_edge, w_msg, w_out, bias_gain, table, lons, *senders.shape)
        own, = near_call(band, rank, lists, w_edge, w_msg, w_out, bias_gain, table, nodes, nodes * lons)
        pairs = lambda k, polar: [
            (j * lats + i, (j ^ k) * lats + i) for i in range(lats) for j in range(lons)
            if not polar or i in (0, lats - 1)]
        got = [lax.ppermute(blocks[k - 1], ('lon', 'lat'), pairs(k, k == 2)) for k in (3, 2, 1)]
        mesh_out = node_call([own] + got, own_vm, w_node, w_out, bias_gain)
        flat = update_call(vg.reshape(batch * rows * cols, latent), w_gupd, w_out, bias_gain, own)
        grid_out = flat.reshape(batch, rows, cols, latent)
        return mesh_out, grid_out

    grid_spec = P('dp', 'lat', 'lon', None)
    node_spec = P(('lat', 'lon'), None)
    slot_spec = P(('lat', 'lon'), None, None)
    in_specs = (grid_spec, node_spec, slot_spec, node_spec, node_spec) + (P(),) * 8
    out_specs = (P('dp', ('lat', 'lon'), None), grid_spec)
    return jax.shard_map(cell_step, mesh=mesh, in_specs=in_specs, out_specs=out_specs, check_vma=False)
```

profile of v0, /device:TPU:0, one launch (start us, length us, event | category | flops | bytes accessed | tf_op | source)
XLA Modules:
  0.0 47.3 jit_solution(2913294869204833462)
XLA Ops:
  0.6 0.0 copy-start.2
  0.6 0.0 copy-start
  0.7 0.0 copy-start.10
  0.7 0.0 copy-start.9
  0.7 0.0 copy-start.8
  0.7 0.0 copy-start.7
  0.7 0.0 copy-start.12
  0.7 0.0 copy-start.3
  0.7 0.0 copy-start.6
  0.7 0.7 %copy-done.2 = f32[6,4,512]{2,1,0:T(4,128)S(1)} copy-done((f32[6,4,512]{2,1,0:T(4,128)S(1)}, f32[6,4,512]{2,1,0:T(4,128)}, u32[]{:S(2)}) %copy-start.2) | copy-done | bytes 49176
  1.4 1.1 %copy-done = bf16[6,512,512]{2,1,0:T(8,128)(2,1)S(1)} copy-done((bf16[6,512,512]{2,1,0:T(8,128)(2,1)S(1)}, bf16[6,512,512]{2,1,0:T(8,128)(2,1)}, u32[]{:S(2)}) %copy-start) | copy-done | bytes 3145752
  2.6 0.0 copy-done.10
  2.6 0.0 copy-done.9
  2.6 0.0 copy-done.8
  2.6 0.0 copy-done.7
  2.6 0.0 copy-done.12
  2.6 0.5 %pack.1 = (bf16[16,512]{1,0:T(8,128)(2,1)S(1)}, f32[8,512]{1,0:T(8,128)S(1)}) custom-call(s32[8,48]{1,0:T(8,128)S(1)} %copy-done.8, s32[8,48]{1,0:T(8,128)S(1)} %copy-done.9, bf16[8,4,48]{2,1,0:T(4,128)(2,1)S(1)} %bitcast.4, bf16[3,8]{1,0:T(4,128)(2,1)S(1)} %bitcast.5, f32[8,128]{1,0:T(8,128)S(1)} %idle.1.dep_ref, bf16[3,512]{1,0:T(4,128)(2,1)S(1)} %copy-done.10, ...), custom_call_target="tpu_custom_call" | custom-call | flops 2000000000 | bytes 1000000 | tf_op jit(solution)/shard_map/pack/pallas_call | solution.py:121
  3.1 0.8 %copy-done.3 = bf16[16,16,16,474]{3,2,1,0:T(8,128)(2,1)S(1)} copy-done((bf16[16,16,16,474]{3,2,1,0:T(8,128)(2,1)S(1)}, bf16[16,16,16,474]{3,2,1,0:T(8,128)(2,1)}, u32[]{:S(2)}) %copy-start.3) | copy-done | bytes 3883032
  3.9 0.0 copy-done.6
  3.9 0.0 copy-start.4
  3.9 0.0 copy-start.11
  3.9 12.4 %embed.1 = (bf16[16,16,16,512]{3,2,1,0:T(8,128)(2,1)S(1)}, bf16[22,16,16,512]{3,2,1,0:T(8,128)(2,1)S(1)}, bf16[4,16,512]{2,1,0:T(8,128)(2,1)S(1)}, f32[32,128]{1,0:T(8,128)S(1)}, f32[32,512]{1,0:T(8,128)S(1)}) custom-call(bf16[16,16,16,474]{3,2,1,0:T(8,128)(2,1)S(1)} %copy-done.3, bf16[474,512]{1,0:T(8,128)(2,1)S(1)} %copy-done.6, ...), custom_call_target="tpu_custom_call" | custom-call | flops 4294967296 | bytes 12582912 | tf_op jit(solution)/shard_map/embed/pallas_call | solution.py:273
  16.4 0.0 copy-done.4
  16.4 0.0 copy-done.11
  16.4 8.4 %edges_far.1 = (f32[8,16,512]{2,1,0:T(8,128)S(1)}, f32[8,16,512]{2,1,0:T(8,128)S(1)}, f32[8,16,512]{2,1,0:T(8,128)S(1)}, s32[1,1792]{1,0:T(1,128)S(1)}, bf16[96,512]{1,0:T(8,128)(2,1)S(1)}) custom-call(bf16[4,16,512]{2,1,0:T(8,128)(2,1)S(1)} %get-tuple-element.16.v_ref, f32[32,128]{1,0:T(8,128)S(1)} %get-tuple-element.17.rank_ref, ...), custom_call_target="tpu_custom_call" | custom-call | flops 3758096384 | bytes 14680064 | tf_op jit(solution)/shard_map/edges_far/pallas_call | solution.py:522
  24.8 2.3 %collective-permute-start = (f32[8,16,512]{2,1,0:T(8,128)S(1)}, f32[8,16,512]{2,1,0:T(8,128)S(1)}, u32[]{:S(2)}, u32[]{:S(2)}) collective-permute-start(f32[8,16,512]{2,1,0:T(8,128)S(1)} %get-tuple-element.22), channel_id=1, source_target_pairs={{0,12},{4,8},{8,4},{12,0},{1,13},{5,9},{9,5},{13,1},{2,14},{6,10},... | collective-permute-start | bytes 786440 | tf_op jit(solution)/shard_map/ppermute | solution.py:607
  27.1 2.1 %collective-permute-start.1 = (f32[8,16,512]{2,1,0:T(8,128)S(1)}, f32[8,16,512]{2,1,0:T(8,128)S(1)}, u32[]{:S(2)}, u32[]{:S(2)}) collective-permute-start(f32[8,16,512]{2,1,0:T(8,128)S(1)} %get-tuple-element.23), channel_id=1, source_target_pairs={{0,8},{4,12},{8,0},{12,4},{3,11},{7,15},{11,3},{15,7},{16,24},{20,... | collective-permute-start | bytes 786440 | tf_op jit(solution)/shard_map/ppermute | solution.py:607
  29.2 2.2 %collective-permute-start.2 = (f32[8,16,512]{2,1,0:T(8,128)S(1)}, f32[8,16,512]{2,1,0:T(8,128)S(1)}, u32[]{:S(2)}, u32[]{:S(2)}) collective-permute-start(f32[8,16,512]{2,1,0:T(8,128)S(1)} %get-tuple-element.24), channel_id=1, source_target_pairs={{0,4},{4,0},{8,12},{12,8},{1,5},{5,1},{9,13},{13,9},{2,6},{6,2},{1... | collective-permute-start | bytes 786440 | tf_op jit(solution)/shard_map/ppermute | solution.py:607
  31.4 0.0 copy-start.5
  31.4 7.2 %edges_near.1.own_ref.dep_ref = f32[8,16,512]{2,1,0:T(8,128)S(1)} custom-call(s32[1,1792]{1,0:T(1,128)S(1)} %get-tuple-element.20.idx, bf16[4,16,512]{2,1,0:T(8,128)(2,1)S(1)} %get-tuple-element.16.v_ref, f32[32,128]{1,0:T(8,128)S(1)} %get-tuple-element.17.rank_ref, bf16[96,512]{1,0:T(8,128)(2,1)S(1)} %get-tuple-element.21.proj_ref, ...), custom_call_target="tpu_custom_call" | custom-call | flops 7516192768 | bytes 14680064 | tf_op jit(solution)/shard_map/edges_near/pallas_call | solution.py:544
  38.6 0.0 copy-done.5
  38.6 0.0 copy-start.1
  38.6 7.3 %update.1 = bf16[4096,512]{1,0:T(8,128)(2,1)} custom-call(bf16[4096,512]{1,0:T(8,128)(2,1)S(1)} %bitcast.6, bf16[512,512]{1,0:T(8,128)(2,1)S(1)} %copy-done.5, bf16[6,512,512]{2,1,0:T(8,128)(2,1)S(1)} %copy-done, f32[6,4,512]{2,1,0:T(4,128)S(1)} %copy-done.2, f32[8,16,512]{2,1,0:T(8,128)S(1)} %edges_near.1.own_ref.dep_ref), custom_call_target="tpu_custom_call" | custom-call | flops 4294967296 | bytes 8388608 | tf_op jit(solution)/shard_map/update/pallas_call | solution.py:341
  45.9 0.0 collective-permute-done.r1_ref
  45.9 0.0 collective-permute-done.1.r2_ref
  45.9 0.0 collective-permute-done.2.r3_ref
  45.9 0.0 copy-done.1
  45.9 1.4 %nodes.1 = bf16[16,8,512]{2,1,0:T(8,128)(2,1)} custom-call(f32[8,16,512]{2,1,0:T(8,128)S(1)} %edges_near.1.own_ref.dep_ref, f32[8,16,512]{2,1,0:T(8,128)S(1)} %collective-permute-done.r1_ref, f32[8,16,512]{2,1,0:T(8,128)S(1)} %collective-permute-done.1.r2_ref, f32[8,16,512]{2,1,0:T(8,128)S(1)} %collective-permute-done.2.r3_ref, ...), custom_call_target="tpu_custom_call" | custom-call | tf_op jit(solution)/shard_map/nodes/pallas_call | solution.py:578
  (1 shorter events, 0.0 us)
Async XLA Ops:
  0.6 0.8 %copy-start.2 = (f32[6,4,512]{2,1,0:T(4,128)S(1)}, f32[6,4,512]{2,1,0:T(4,128)}, u32[]{:S(2)}) copy-start(f32[6,4,512]{2,1,0:T(4,128)} %bg_ref.11) | copy-start | bytes 147460
  0.6 1.9 %copy-start = (bf16[6,512,512]{2,1,0:T(8,128)(2,1)S(1)}, bf16[6,512,512]{2,1,0:T(8,128)(2,1)}, u32[]{:S(2)}) copy-start(bf16[6,512,512]{2,1,0:T(8,128)(2,1)} %wo_ref.9) | copy-start | bytes 9437188
  0.7 1.9 %copy-start.10 = (bf16[3,512]{1,0:T(4,128)(2,1)S(1)}, bf16[3,512]{1,0:T(4,128)(2,1)}, u32[]{:S(2)}) copy-start(bf16[3,512]{1,0:T(4,128)(2,1)} %wm_ref.1) | copy-start | bytes 9220
  0.7 1.9 %copy-start.9 = (s32[8,48]{1,0:T(8,128)S(1)}, s32[8,48]{1,0:T(8,128)}, u32[]{:S(2)}) copy-start(s32[8,48]{1,0:T(8,128)} %mask_ref.1) | copy-start | bytes 4612
  0.7 1.9 %copy-start.8 = (s32[8,48]{1,0:T(8,128)S(1)}, s32[8,48]{1,0:T(8,128)}, u32[]{:S(2)}) copy-start(s32[8,48]{1,0:T(8,128)} %send_ref.1) | copy-start | bytes 4612
  0.7 1.9 %copy-start.7 = (bf16[8,48,4]{1,2,0:T(4,128)(2,1)S(1)}, bf16[8,48,4]{1,2,0:T(4,128)(2,1)}, u32[]{:S(2)}) copy-start(bf16[8,48,4]{1,2,0:T(4,128)(2,1)} %param.15) | copy-start | bytes 9220
  0.7 1.9 %copy-start.12 = (bf16[8,3]{0,1:T(4,128)(2,1)S(1)}, bf16[8,3]{0,1:T(4,128)(2,1)}, u32[]{:S(2)}) copy-start(bf16[8,3]{0,1:T(4,128)(2,1)} %param.14) | copy-start | bytes 148
  0.7 3.2 %copy-start.3 = (bf16[16,16,16,474]{3,2,1,0:T(8,128)(2,1)S(1)}, bf16[16,16,16,474]{3,2,1,0:T(8,128)(2,1)}, u32[]{:S(2)}) copy-start(bf16[16,16,16,474]{3,2,1,0:T(8,128)(2,1)} %x_ref.1) | copy-start | bytes 11649028
  0.7 3.2 %copy-start.6 = (bf16[474,512]{1,0:T(8,128)(2,1)S(1)}, bf16[474,512]{1,0:T(8,128)(2,1)}, u32[]{:S(2)}) copy-start(bf16[474,512]{1,0:T(8,128)(2,1)} %wg_ref.1) | copy-start | bytes 1456132
  3.9 12.5 %copy-start.4 = (bf16[1536,512]{1,0:T(8,128)(2,1)S(1)}, bf16[1536,512]{1,0:T(8,128)(2,1)}, u32[]{:S(2)}) copy-start(bf16[1536,512]{1,0:T(8,128)(2,1)} %wmsg_ref.3) | copy-start | bytes 4718596
  3.9 12.5 %copy-start.11 = (bf16[4,512]{1,0:T(4,128)(2,1)S(1)}, bf16[4,512]{1,0:T(4,128)(2,1)}, u32[]{:S(2)}) copy-start(bf16[4,512]{1,0:T(4,128)(2,1)} %we_ref.3) | copy-start | bytes 12292
  24.8 21.1 %collective-permute-start = (f32[8,16,512]{2,1,0:T(8,128)S(1)}, f32[8,16,512]{2,1,0:T(8,128)S(1)}, u32[]{:S(2)}, u32[]{:S(2)}) collective-permute-start(f32[8,16,512]{2,1,0:T(8,128)S(1)} %get-tuple-element.22), channel_id=1, source_target_pairs={{0,12},{4,8},{8,4},{12,0},{1,13},{5,9},{9,5},{13,1},{2,14},{6,10},... | collective-permute-start | bytes 786440 | tf_op jit(solution)/shard_map/ppermute | solution.py:607
  27.1 18.8 %collective-permute-start.1 = (f32[8,16,512]{2,1,0:T(8,128)S(1)}, f32[8,16,512]{2,1,0:T(8,128)S(1)}, u32[]{:S(2)}, u32[]{:S(2)}) collective-permute-start(f32[8,16,512]{2,1,0:T(8,128)S(1)} %get-tuple-element.23), channel_id=1, source_target_pairs={{0,8},{4,12},{8,0},{12,4},{3,11},{7,15},{11,3},{15,7},{16,24},{20,... | collective-permute-start | bytes 786440 | tf_op jit(solution)/shard_map/ppermute | solution.py:607
  29.2 16.7 %collective-permute-start.2 = (f32[8,16,512]{2,1,0:T(8,128)S(1)}, f32[8,16,512]{2,1,0:T(8,128)S(1)}, u32[]{:S(2)}, u32[]{:S(2)}) collective-permute-start(f32[8,16,512]{2,1,0:T(8,128)S(1)} %get-tuple-element.24), channel_id=1, source_target_pairs={{0,4},{4,0},{8,12},{12,8},{1,5},{5,1},{9,13},{13,9},{2,6},{6,2},{1... | collective-permute-start | bytes 786440 | tf_op jit(solution)/shard_map/ppermute | solution.py:607
  31.4 7.2 %copy-start.5 = (bf16[512,512]{1,0:T(8,128)(2,1)S(1)}, bf16[512,512]{1,0:T(8,128)(2,1)}, u32[]{:S(2)}) copy-start(bf16[512,512]{1,0:T(8,128)(2,1)} %wu_ref.1) | copy-start | bytes 1572868
  38.6 7.3 %copy-start.1 = (bf16[1024,512]{1,0:T(8,128)(2,1)S(1)}, bf16[1024,512]{1,0:T(8,128)(2,1)}, u32[]{:S(2)}) copy-start(bf16[1024,512]{1,0:T(8,128)(2,1)} %wn_ref.1) | copy-start | bytes 3145732
where the time goes:
time: 47.9 us; the launch traced here: 47.3 us
  Pallas kernels  37.2 us (78%)
  starting transfers between devices  6.59 us (14%)
  local copies, waits for them, and re-layouts  2.69 us (6%)
  between operations  0.84 us (2%)
    pallas_call x1, Pallas kernels, embed_call(): pl.pallas_call(functools.partial(embed_kernel, lats=lats, lons=lons), in_...  12.4 us
    pallas_call x1, Pallas kernels, edge_call(): pl.pallas_call(functools.partial(far_kernel, lons=lons, nodes=nodes), in_...  8.38 us
    pallas_call x1, Pallas kernels, update_call(): pl.pallas_call(update_kernel, in_specs=[local] * 4 + [anywhere], out_spec...  7.28 us
    pallas_call x1, Pallas kernels, near_call(): pl.pallas_call(near_kernel, in_specs=[pl.BlockSpec(memory_space=pltpu.SME...  7.17 us
    ppermute x3, starting transfers between devices, cell_step(): lax.ppermute(blocks[k - 1], ('lon', 'lat'), pairs(k, k == 2))  6.59 us
    unnamed x26, local copies, waits for them, and re-layouts  2.69 us
    pallas_call x1, Pallas kernels, node_call(): pl.pallas_call(node_kernel, in_specs=[local] * 8, out_specs=local, out_sh...  1.4 us
  transfers between devices with their start and end apart: 3, of which 0 were waited for; matrix products, arithmetic and copies ran while one was open for 0% of the time, Pallas kernels for 31%

commit v1 on v0

--- a/solution.py
+++ b/solution.py
@@ -604,7 +604,9 @@
         pairs = lambda k, polar: [
             (j * lats + i, (j ^ k) * lats + i) for i in range(lats) for j in range(lons)
             if not polar or i in (0, lats - 1)]
-        got = [lax.ppermute(blocks[k - 1], ('lon', 'lat'), pairs(k, k == 2)) for k in (3, 2, 1)]
+        last_block, own = lax.optimization_barrier((blocks[0], own))
+        sends = ((3, blocks[2]), (2, blocks[1]), (1, last_block))
+        got = [lax.ppermute(block, ('lon', 'lat'), pairs(k, k == 2)) for k, block in sends]
         mesh_out = node_call([own] + got, own_vm, w_node, w_out, bias_gain)
         flat = update_call(vg.reshape(batch * rows * cols, latent), w_gupd, w_out, bias_gain, own)
         grid_out = flat.reshape(batch, rows, cols, latent)

time: 47.9 us -> 54.1 us (1.13)
  waiting for transfers between devices: 0.01 us -> 7.32 us
  Pallas kernels: 37.2 us -> 34 us
  starting transfers between devices: 6.59 us -> 8.69 us
    ppermute x3, waiting for transfers between devices: 0.01 us -> 7.32 us  [cell_step(): lax.ppermute(block, ('lon', 'lat'), pairs(k, k == 2))]
    ppermute x3, starting transfers between devices: 6.59 us -> 8.69 us  [cell_step(): lax.ppermute(block, ('lon', 'lat'), pairs(k, k == 2))]
    pallas_call x1, Pallas kernels: 8.38 us -> 6.35 us  [edge_call(): pl.pallas_call(functools.partial(far_kernel, lons=lons, nodes=nodes), in_...]
    pallas_call x1, Pallas kernels: 7.17 us -> 6 us  [near_call(): pl.pallas_call(near_kernel, in_specs=[pl.BlockSpec(memory_space=pltpu.SME...]
  transfers between devices with their start and end apart: 3 -> 3, of which waited for: 0 -> 2; matrix products, arithmetic and copies ran while one was open for 0% -> 0% of each run, Pallas kernels for 31% -> 14%
where the time goes in v1:
time: 54.1 us; the launch traced here: 53.5 us
  Pallas kernels  34 us (63%)
  starting transfers between devices  8.69 us (16%)
  waiting for transfers between devices  7.32 us (14%)
  local copies, waits for them, and re-layouts  2.7 us (5%)
  between operations  0.82 us (2%)
    pallas_call x1, Pallas kernels, embed_call(): pl.pallas_call(functools.partial(embed_kernel, lats=lats, lons=lons), in_...  12.4 us
    ppermute x3, starting transfers between devices, cell_step(): lax.ppermute(block, ('lon', 'lat'), pairs(k, k == 2))  8.69 us
    ppermute x3, waiting for transfers between devices, cell_step(): lax.ppermute(block, ('lon', 'lat'), pairs(k, k == 2))  7.32 us
    pallas_call x1, Pallas kernels, update_call(): pl.pallas_call(update_kernel, in_specs=[local] * 4 + [anywhere], out_spec...  7.28 us
    pallas_call x1, Pallas kernels, edge_call(): pl.pallas_call(functools.partial(far_kernel, lons=lons, nodes=nodes), in_...  6.35 us
    pallas_call x1, Pallas kernels, near_call(): pl.pallas_call(near_kernel, in_specs=[pl.BlockSpec(memory_space=pltpu.SME...  6 us
    unnamed x26, local copies, waits for them, and re-layouts  2.7 us
    pallas_call x1, Pallas kernels, node_call(): pl.pallas_call(node_kernel, in_specs=[local] * 8, out_specs=local, out_sh...  1.4 us
  transfers between devices with their start and end apart: 3, of which 2 were waited for; matrix products, arithmetic and copies ran while one was open for 0% of the time, Pallas kernels for 14%

profile of v1, /device:TPU:0, one launch (start us, length us, event | category | flops | bytes accessed | tf_op | source)
XLA Modules:
  0.0 53.5 jit_solution(7529448164884322753)
XLA Ops:
  0.6 0.0 copy-start.2
  0.6 0.0 copy-start
  0.7 0.0 copy-start.10
  0.7 0.0 copy-start.9
  0.7 0.0 copy-start.8
  0.7 0.0 copy-start.7
  0.7 0.0 copy-start.12
  0.7 0.0 copy-start.3
  0.7 0.0 copy-start.6
  0.7 0.7 %copy-done.2 = f32[6,4,512]{2,1,0:T(4,128)S(1)} copy-done((f32[6,4,512]{2,1,0:T(4,128)S(1)}, f32[6,4,512]{2,1,0:T(4,128)}, u32[]{:S(2)}) %copy-start.2) | copy-done | bytes 49176
  1.4 1.1 %copy-done = bf16[6,512,512]{2,1,0:T(8,128)(2,1)S(1)} copy-done((bf16[6,512,512]{2,1,0:T(8,128)(2,1)S(1)}, bf16[6,512,512]{2,1,0:T(8,128)(2,1)}, u32[]{:S(2)}) %copy-start) | copy-done | bytes 3145752
  2.6 0.0 copy-done.10
  2.6 0.0 copy-done.9
  2.6 0.0 copy-done.8
  2.6 0.0 copy-done.7
  2.6 0.0 copy-done.12
  2.6 0.5 pack.1
  3.1 0.8 %copy-done.3 = bf16[16,16,16,474]{3,2,1,0:T(8,128)(2,1)S(1)} copy-done((bf16[16,16,16,474]{3,2,1,0:T(8,128)(2,1)S(1)}, bf16[16,16,16,474]{3,2,1,0:T(8,128)(2,1)}, u32[]{:S(2)}) %copy-start.3) | copy-done | bytes 3883032
  3.9 0.0 copy-done.6
  3.9 0.0 copy-start.4
  3.9 0.0 copy-start.11
  3.9 12.4 %embed.1 = (bf16[16,16,16,512]{3,2,1,0:T(8,128)(2,1)S(1)}, bf16[22,16,16,512]{3,2,1,0:T(8,128)(2,1)S(1)}, bf16[4,16,512]{2,1,0:T(8,128)(2,1)S(1)}, f32[32,128]{1,0:T(8,128)S(1)}, f32[32,512]{1,0:T(8,128)S(1)}) custom-call(bf16[16,16,16,474]{3,2,1,0:T(8,128)(2,1)S(1)} %copy-done.3, bf16[474,512]{1,0:T(8,128)(2,1)S(1)} %copy-done.6, ...), custom_call_target="tpu_custom_call" | custom-call | flops 4294967296 | bytes 12582912 | tf_op jit(solution)/shard_map/embed/pallas_call | solution.py:273
  16.4 0.0 copy-done.4
  16.4 0.0 copy-done.11
  16.4 6.3 %edges_far.1 = (f32[8,16,512]{2,1,0:T(8,128)S(1)}, f32[8,16,512]{2,1,0:T(8,128)S(1)}, f32[8,16,512]{2,1,0:T(8,128)S(1)}, s32[1,1792]{1,0:T(1,128)S(1)}, bf16[96,512]{1,0:T(8,128)(2,1)S(1)}) custom-call(bf16[4,16,512]{2,1,0:T(8,128)(2,1)S(1)} %get-tuple-element.18.v_ref, f32[32,128]{1,0:T(8,128)S(1)} %get-tuple-element.19.rank_ref, ...), custom_call_target="tpu_custom_call" | custom-call | flops 3758096384 | bytes 14680064 | tf_op jit(solution)/shard_map/edges_far/pallas_call | solution.py:522
  22.8 0.0 copy-start.5
  22.8 6.0 %edges_near.1.own_ref.dep_ref = f32[8,16,512]{2,1,0:T(8,128)S(1)} custom-call(s32[1,1792]{1,0:T(1,128)S(1)} %get-tuple-element.23.idx, bf16[4,16,512]{2,1,0:T(8,128)(2,1)S(1)} %get-tuple-element.18.v_ref, f32[32,128]{1,0:T(8,128)S(1)} %get-tuple-element.19.rank_ref, bf16[96,512]{1,0:T(8,128)(2,1)S(1)} %get-tuple-element.24.proj_ref, ...), custom_call_target="tpu_custom_call" | custom-call | flops 7516192768 | bytes 14680064 | tf_op jit(solution)/shard_map/edges_near/pallas_call | solution.py:544
  28.8 3.0 %collective-permute-start.2 = (f32[8,16,512]{2,1,0:T(8,128)S(1)}, f32[8,16,512]{2,1,0:T(8,128)S(1)}, u32[]{:S(2)}, u32[]{:S(2)}) collective-permute-start(f32[8,16,512]{2,1,0:T(8,128)S(1)} %get-tuple-element.28), channel_id=1, source_target_pairs={{0,4},{4,0},{8,12},{12,8},{1,5},{5,1},{9,13},{13,9},{2,6},{6,2},{1... | collective-permute-start | bytes 786440 | tf_op jit(solution)/shard_map/ppermute | solution.py:609
  31.8 3.7 %collective-permute-start = (f32[8,16,512]{2,1,0:T(8,128)S(1)}, f32[8,16,512]{2,1,0:T(8,128)S(1)}, u32[]{:S(2)}, u32[]{:S(2)}) collective-permute-start(f32[8,16,512]{2,1,0:T(8,128)S(1)} %get-tuple-element.26), channel_id=1, source_target_pairs={{0,12},{4,8},{8,4},{12,0},{1,13},{5,9},{9,5},{13,1},{2,14},{6,10},... | collective-permute-start | bytes 786440 | tf_op jit(solution)/shard_map/ppermute | solution.py:609
  35.5 1.9 %collective-permute-start.1 = (f32[8,16,512]{2,1,0:T(8,128)S(1)}, f32[8,16,512]{2,1,0:T(8,128)S(1)}, u32[]{:S(2)}, u32[]{:S(2)}) collective-permute-start(f32[8,16,512]{2,1,0:T(8,128)S(1)} %get-tuple-element.27), channel_id=1, source_target_pairs={{0,8},{4,12},{8,0},{12,4},{3,11},{7,15},{11,3},{15,7},{16,24},{20,... | collective-permute-start | bytes 786440 | tf_op jit(solution)/shard_map/ppermute | solution.py:609
  37.5 0.0 copy-done.5
  37.5 0.0 copy-start.1
  37.5 7.3 %update.1 = bf16[4096,512]{1,0:T(8,128)(2,1)} custom-call(bf16[4096,512]{1,0:T(8,128)(2,1)S(1)} %bitcast.6, bf16[512,512]{1,0:T(8,128)(2,1)S(1)} %copy-done.5, bf16[6,512,512]{2,1,0:T(8,128)(2,1)S(1)} %copy-done, f32[6,4,512]{2,1,0:T(4,128)S(1)} %copy-done.2, f32[8,16,512]{2,1,0:T(8,128)S(1)} %edges_near.1.own_ref.dep_ref), custom_call_target="tpu_custom_call" | custom-call | flops 4294967296 | bytes 8388608 | tf_op jit(solution)/shard_map/update/pallas_call | solution.py:341
  44.8 0.0 collective-permute-done.2.r3_ref
  44.8 1.7 %collective-permute-done.r1_ref = f32[8,16,512]{2,1,0:T(8,128)S(1)} collective-permute-done((f32[8,16,512]{2,1,0:T(8,128)S(1)}, f32[8,16,512]{2,1,0:T(8,128)S(1)}, u32[]{:S(2)}, u32[]{:S(2)}) %collective-permute-start) | collective-permute-done | bytes 262176 | tf_op jit(solution)/shard_map/ppermute | solution.py:609
  46.5 5.6 %collective-permute-done.1.r2_ref = f32[8,16,512]{2,1,0:T(8,128)S(1)} collective-permute-done((f32[8,16,512]{2,1,0:T(8,128)S(1)}, f32[8,16,512]{2,1,0:T(8,128)S(1)}, u32[]{:S(2)}, u32[]{:S(2)}) %collective-permute-start.1) | collective-permute-done | bytes 262176 | tf_op jit(solution)/shard_map/ppermute | solution.py:609
  52.1 0.0 copy-done.1
  52.1 1.4 %nodes.1 = bf16[16,8,512]{2,1,0:T(8,128)(2,1)} custom-call(f32[8,16,512]{2,1,0:T(8,128)S(1)} %edges_near.1.own_ref.dep_ref, f32[8,16,512]{2,1,0:T(8,128)S(1)} %collective-permute-done.r1_ref, f32[8,16,512]{2,1,0:T(8,128)S(1)} %collective-permute-done.1.r2_ref, f32[8,16,512]{2,1,0:T(8,128)S(1)} %collective-permute-done.2.r3_ref, ...), custom_call_target="tpu_custom_call" | custom-call | tf_op jit(solution)/shard_map/nodes/pallas_call | solution.py:578
  (1 shorter events, 0.0 us)
Async XLA Ops:
  0.6 0.8 %copy-start.2 = (f32[6,4,512]{2,1,0:T(4,128)S(1)}, f32[6,4,512]{2,1,0:T(4,128)}, u32[]{:S(2)}) copy-start(f32[6,4,512]{2,1,0:T(4,128)} %bg_ref.11) | copy-start | bytes 147460
  0.6 1.9 %copy-start = (bf16[6,512,512]{2,1,0:T(8,128)(2,1)S(1)}, bf16[6,512,512]{2,1,0:T(8,128)(2,1)}, u32[]{:S(2)}) copy-start(bf16[6,512,512]{2,1,0:T(8,128)(2,1)} %wo_ref.9) | copy-start | bytes 9437188
  0.7 1.9 %copy-start.10 = (bf16[3,512]{1,0:T(4,128)(2,1)S(1)}, bf16[3,512]{1,0:T(4,128)(2,1)}, u32[]{:S(2)}) copy-start(bf16[3,512]{1,0:T(4,128)(2,1)} %wm_ref.1) | copy-start | bytes 9220
  0.7 1.9 %copy-start.9 = (s32[8,48]{1,0:T(8,128)S(1)}, s32[8,48]{1,0:T(8,128)}, u32[]{:S(2)}) copy-start(s32[8,48]{1,0:T(8,128)} %mask_ref.1) | copy-start | bytes 4612
  0.7 1.9 %copy-start.8 = (s32[8,48]{1,0:T(8,128)S(1)}, s32[8,48]{1,0:T(8,128)}, u32[]{:S(2)}) copy-start(s32[8,48]{1,0:T(8,128)} %send_ref.1) | copy-start | bytes 4612
  0.7 1.9 %copy-start.7 = (bf16[8,48,4]{1,2,0:T(4,128)(2,1)S(1)}, bf16[8,48,4]{1,2,0:T(4,128)(2,1)}, u32[]{:S(2)}) copy-start(bf16[8,48,4]{1,2,0:T(4,128)(2,1)} %param.15) | copy-start | bytes 9220
  0.7 1.9 %copy-start.12 = (bf16[8,3]{0,1:T(4,128)(2,1)S(1)}, bf16[8,3]{0,1:T(4,128)(2,1)}, u32[]{:S(2)}) copy-start(bf16[8,3]{0,1:T(4,128)(2,1)} %param.14) | copy-start | bytes 148
  0.7 3.2 %copy-start.3 = (bf16[16,16,16,474]{3,2,1,0:T(8,128)(2,1)S(1)}, bf16[16,16,16,474]{3,2,1,0:T(8,128)(2,1)}, u32[]{:S(2)}) copy-start(bf16[16,16,16,474]{3,2,1,0:T(8,128)(2,1)} %x_ref.1) | copy-start | bytes 11649028
  0.7 3.2 %copy-start.6 = (bf16[474,512]{1,0:T(8,128)(2,1)S(1)}, bf16[474,512]{1,0:T(8,128)(2,1)}, u32[]{:S(2)}) copy-start(bf16[474,512]{1,0:T(8,128)(2,1)} %wg_ref.1) | copy-start | bytes 1456132
  3.9 12.5 %copy-start.4 = (bf16[1536,512]{1,0:T(8,128)(2,1)S(1)}, bf16[1536,512]{1,0:T(8,128)(2,1)}, u32[]{:S(2)}) copy-start(bf16[1536,512]{1,0:T(8,128)(2,1)} %wmsg_ref.3) | copy-start | bytes 4718596
  3.9 12.5 %copy-start.11 = (bf16[4,512]{1,0:T(4,128)(2,1)S(1)}, bf16[4,512]{1,0:T(4,128)(2,1)}, u32[]{:S(2)}) copy-start(bf16[4,512]{1,0:T(4,128)(2,1)} %we_ref.3) | copy-start | bytes 12292
  22.8 14.7 %copy-start.5 = (bf16[512,512]{1,0:T(8,128)(2,1)S(1)}, bf16[512,512]{1,0:T(8,128)(2,1)}, u32[]{:S(2)}) copy-start(bf16[512,512]{1,0:T(8,128)(2,1)} %wu_ref.1) | copy-start | bytes 1572868
  28.8 16.0 %collective-permute-start.2 = (f32[8,16,512]{2,1,0:T(8,128)S(1)}, f32[8,16,512]{2,1,0:T(8,128)S(1)}, u32[]{:S(2)}, u32[]{:S(2)}) collective-permute-start(f32[8,16,512]{2,1,0:T(8,128)S(1)} %get-tuple-element.28), channel_id=1, source_target_pairs={{0,4},{4,0},{8,12},{12,8},{1,5},{5,1},{9,13},{13,9},{2,6},{6,2},{1... | collective-permute-start | bytes 786440 | tf_op jit(solution)/shard_map/ppermute | solution.py:609
  31.8 14.7 %collective-permute-start = (f32[8,16,512]{2,1,0:T(8,128)S(1)}, f32[8,16,512]{2,1,0:T(8,128)S(1)}, u32[]{:S(2)}, u32[]{:S(2)}) collective-permute-start(f32[8,16,512]{2,1,0:T(8,128)S(1)} %get-tuple-element.26), channel_id=1, source_target_pairs={{0,12},{4,8},{8,4},{12,0},{1,13},{5,9},{9,5},{13,1},{2,14},{6,10},... | collective-permute-start | bytes 786440 | tf_op jit(solution)/shard_map/ppermute | solution.py:609
  35.5 16.6 %collective-permute-start.1 = (f32[8,16,512]{2,1,0:T(8,128)S(1)}, f32[8,16,512]{2,1,0:T(8,128)S(1)}, u32[]{:S(2)}, u32[]{:S(2)}) collective-permute-start(f32[8,16,512]{2,1,0:T(8,128)S(1)} %get-tuple-element.27), channel_id=1, source_target_pairs={{0,8},{4,12},{8,0},{12,4},{3,11},{7,15},{11,3},{15,7},{16,24},{20,... | collective-permute-start | bytes 786440 | tf_op jit(solution)/shard_map/ppermute | solution.py:609
  37.5 14.6 %copy-start.1 = (bf16[1024,512]{1,0:T(8,128)(2,1)S(1)}, bf16[1024,512]{1,0:T(8,128)(2,1)}, u32[]{:S(2)}) copy-start(bf16[1024,512]{1,0:T(8,128)(2,1)} %wn_ref.1) | copy-start | bytes 3145732
